TPU v7x, 256 devices: a whole 4x4x8 slice. The times are simulated.
256 devices in a mesh: shot: 8 (over x_hi, y), rcv: 32 (over x_lo, z, core).
Axes of the slice: x: 4 (x_hi: 2, x_lo: 2; x = x_hi * 2 + x_lo), y: 4, z: 8, core: 2. Of those that a mesh axis runs over, the one named last changes fastest.
Arguments:
- modeled: bfloat16 [2, 64, 8, 256, 512], P(None, 'shot', None, 'rcv'), may hold values from -9 to 9
- observed: bfloat16 [2, 8, 64, 256, 512], P(None, 'shot', 'rcv'), may hold values from -60 to 60
- mask: int32 [64, 8, 256], P('shot', None, 'rcv'), may hold values 0 or 1
- shot_order: int32 [64], replicated, may hold values from 0 to 63, as said below
- line_of_slot: int32 [8], replicated, may hold values from 0 to 7, as said below
- coupling: bfloat16 [2, 512, 512], replicated, may hold values from -0.25 to 0.25
- wavelet: float32 [2, 512], replicated, may hold values from -4 to 4
- damping: float32 [512], replicated, may hold values from 32768 to 524288
Outputs:
- new_wavelet: float32 [2, 512], replicated
- residual_out: bfloat16 [2, 64, 8, 256, 512], P(None, 'shot', None, 'rcv')
Inputs may be any that keep to these rules, and one draw needn't show every extreme that they name: Group g holds the shots shot_order[g * 8] to shot_order[(g + 1) * 8 - 1]; each shot number appears once. `line_of_slot`: each line appears in exactly one slot.
All inputs are finite; a program needn't handle non-finite values. No bound on the sum of `mask` on one device may be relied on, other than what follows from the above.
Results may differ from a plain program's by a relative error of at most 0.00045.
Values may be sent and summed in bfloat16 or wider, within the bound.
No kernel may reach another device: no remote copies, remote signals or barrier semaphores. Data moves between devices by JAX's collectives and lax.ppermute only.
A program may use at most 64 MiB of HBM per device.

v0:
```python
import jax
import jax.numpy as jnp
from jax import lax
from jax.experimental import pallas as pl
from jax.experimental.pallas import tpu as pltpu
from jax.sharding import Mesh, PartitionSpec as P

F32 = jnp.float32
BF16 = jnp.bfloat16
SHOT = ("xh", "yh", "yl")
RCV = ("xl", "zh", "zm", "zl", "c")
REST = ("xh", "yh", "yl", "xl")
PILE = ("zh", "zm", "zl", "c")
SWAPS = (4, 5, 6, 7, 1, 2, 3)

VM = pl.BlockSpec(memory_space=pltpu.VMEM)
SM = pl.BlockSpec(memory_space=pltpu.SMEM)
ANY = pl.BlockSpec(memory_space=pl.ANY)
HBM = pl.BlockSpec(memory_space=pltpu.HBM)


def call(body, outs, in_specs, out_specs=None, scratch=(), limit=12 << 20, flops=0, nbytes=1 << 20):
    many = isinstance(outs, (tuple, list))
    return pl.pallas_call(
        body,
        out_shape=outs,
        in_specs=in_specs,
        out_specs=out_specs if out_specs is not None else ([VM] * len(outs) if many else VM),
        scratch_shapes=list(scratch),
        compiler_params=pltpu.CompilerParams(vmem_limit_bytes=limit),
        cost_estimate=pl.CostEstimate(flops=flops, bytes_accessed=nbytes, transcendentals=0),
    )


CHUNKS = 4
BIG = 62 << 20
WIN = 61 << 20
CRS = 50 << 20
GRP = 51 << 20
FIN = 50 << 20


def k_spread(obs_ref, out_ref, buf, sem_in, sem_out):
    parts, pieces = obs_ref.shape[:2]
    held = parts // 2
    step = pieces // CHUNKS
    ins, outs = [], []
    for q in range(CHUNKS):
        rows = pl.ds(q * step, step)
        for i in range(parts):
            to = i % held * 2 + i // held
            ins.append(pltpu.make_async_copy(obs_ref.at[i, rows], buf.at[rows, to], sem_in.at[q, i]))
        outs.append(pltpu.make_async_copy(buf.at[rows], out_ref.at[rows], sem_out.at[q]))
    for c in ins:
        c.start()
    for q in range(CHUNKS):
        for i in range(parts):
            ins[q * parts + i].wait()
        outs[q].start()
    for c in outs:
        c.wait()


def couple(c_ref, b_ref):
    f = c_ref.shape[1]
    re, im = c_ref[0], c_ref[1]
    b_ref[0, :f] = re
    b_ref[0, f:] = -im
    b_ref[1, :f] = im
    b_ref[1, f:] = re


def k_mask(me_ref, slot_ref, mod_ref, mask_ref, live_ref, *out_refs):
    me = me_ref[0]
    shots, rb = mod_ref.shape[1], mod_ref.shape[3]
    f = mod_ref.shape[4]
    eye = lax.broadcasted_iota(jnp.int32, (rb, rb), 0) == lax.broadcasted_iota(jnp.int32, (rb, rb), 1)
    for b, out_ref in enumerate(out_refs):
        line = slot_ref[lax.bitwise_xor(me, b)]
        for s in range(shots):
            row = mask_ref[s, pl.ds(line, 1)].astype(F32)
            column = jnp.where(eye, row, 0.0).sum(axis=1, keepdims=True)
            rows = pl.ds(s * rb, rb)
            live_ref[b, rows] = jnp.broadcast_to(column, (rb, 128))
            live = jnp.broadcast_to(column, (rb, f)) > 0.5
            for c in range(2):
                x = mod_ref[c, s, line].astype(F32)
                out_ref[c, rows] = jnp.where(live, x, 0.0).astype(BF16)


def window(x_ref, b_ref, d):
    x = jnp.concatenate([x_ref[0], x_ref[1]], axis=1)
    return jnp.dot(x, b_ref[d], preferred_element_type=F32)


def window_out(x_ref, b_ref, out_ref, buf, sem):
    copies = []
    for d in range(2):
        buf[d] = window(x_ref, b_ref, d).reshape(buf.shape[1:])
        copies.append(pltpu.make_async_copy(buf.at[d], out_ref.at[d], sem.at[d]))
        if d:
            copies[d - 1].start()
    copies[-1].start()
    for c in copies:
        c.wait()


def k_window(*refs):
    xs, c_ref, (out_ref, coup, x_ref, b_ref, buf, csem, isem, sem) = refs[:-9], refs[-9], refs[-8:]
    rows = xs[0].shape[1]
    first = pltpu.make_async_copy(c_ref, coup, csem)
    first.start()
    ins = [
        pltpu.make_async_copy(x, x_ref.at[:, pl.ds(b * rows, rows)], isem.at[b])
        for b, x in enumerate(xs)
    ]
    for c in ins:
        c.start()
    first.wait()
    couple(coup, b_ref)
    for c in ins:
        c.wait()
    window_out(x_ref, b_ref, out_ref, buf, sem)


def fold(x):
    return x.reshape(x.shape[0] // 8, 8, x.shape[1]).sum(axis=0).sum(axis=0, keepdims=True)


def k_group(me_ref, order_ref, own_ref, send_ref, keep_ref, buf, sem):
    me = me_ref[0]
    half, _, rows, _ = send_ref.shape
    rb = own_ref.shape[3]
    size = rows // rb
    copies = [pltpu.make_async_copy(buf.at[d], send_ref.at[d], sem.at[d]) for d in range(half)]
    for first, to in ((half, buf), (0, keep_ref)):
        for d in range(half):
            g = lax.bitwise_xor(me, first + d)
            for s in range(size):
                n = order_ref[g * size + s]
                j = lax.shift_right_logical(n, 1)
                h = lax.bitwise_and(n, 1)
                for c in range(2):
                    to[d, c, s * rb : (s + 1) * rb] = own_ref[j, h, c]
            if first and d:
                copies[d - 1].start()
        if first:
            copies[-1].start()
    for c in copies:
        c.wait()


def k_pair(keep_ref, came_ref, *refs):
    out_refs, sem = refs[:-1], refs[-1]
    copies = [
        pltpu.make_async_copy(src.at[d], out_ref.at[i], sem.at[i, d])
        for i, src in ((1, came_ref), (0, keep_ref))
        for d, out_ref in enumerate(out_refs)
    ]
    for c in copies:
        c.start()
    for c in copies:
        c.wait()


def k_cross(me_ref, order_ref, own_ref, c_ref, *refs):
    mods, (sum_ref, x_ref, m_ref, b_ref, sem) = refs[:-5], refs[-5:]
    me = me_ref[0]
    groups = len(mods)
    rows, f = mods[0].shape[1:]
    rb = own_ref.shape[3]
    size = rows // rb
    copies = [
        pltpu.make_async_copy(mods[b], m_ref.at[:, pl.ds(b * rows, rows)], sem.at[b])
        for b in range(groups)
    ]
    for c in copies:
        c.start()

    def couple_rows(i, carry):
        block = f // 4
        upper, lower = pl.ds(pl.multiple_of(i * block, block), block), pl.ds(pl.multiple_of(f + i * block, block), block)
        re, im = c_ref[0, upper], c_ref[1, upper]
        b_ref[0, upper] = re
        b_ref[0, lower] = -im
        b_ref[1, upper] = im
        b_ref[1, lower] = re
        return carry

    lax.fori_loop(0, 4, couple_rows, 0)
    for b in range(groups):
        g = lax.bitwise_xor(me, b)
        for s in range(size):
            n = order_ref[g * size + s]
            j = lax.shift_right_logical(n, 1)
            h = lax.bitwise_and(n, 1)
            row = (b * size + s) * rb
            for c in range(2):
                x_ref[c, row : row + rb] = own_ref[j, h, c]
    wd_re, wd_im = window(x_ref, b_ref, 0), window(x_ref, b_ref, 1)
    for c in copies:
        c.wait()
    wg_re, wg_im = window(m_ref, b_ref, 0), window(m_ref, b_ref, 1)
    sum_ref[0:1] = fold(wg_re * wd_re + wg_im * wd_im)
    sum_ref[1:2] = fold(wg_re * wd_im - wg_im * wd_re)
    sum_ref[2:3] = fold(wg_re * wg_re + wg_im * wg_im)


def k_final(me_ref, slot_ref, *refs):
    pairs, refs = refs[:4], refs[4:]
    live_ref, c_ref, wg_ref, sums_ref, wav_ref, damp_ref, nw_ref, out_ref = refs[:8]
    own, live, coup, x_ref, b_ref, wd, wg, buf, nw, psem, lsem, sem, osem, nsem = refs[8:]
    me = me_ref[0]
    _, lines, rows, f = wg_ref.shape
    shots, rb = out_ref.shape[1], out_ref.shape[3]
    half = len(pairs)
    first = [pltpu.make_async_copy(c_ref, coup, lsem.at[0]), pltpu.make_async_copy(live_ref, live, lsem.at[1])]
    first += [pltpu.make_async_copy(p, own.at[d], psem.at[d]) for d, p in enumerate(pairs)]
    ins = [pltpu.make_async_copy(wg_ref.at[:, b], wg.at[:, b], sem.at[b]) for b in range(lines)]
    for c in first + ins:
        c.start()
    for c in first:
        c.wait()

    def couple_rows(i, carry):
        block = f // 4
        upper, lower = pl.ds(pl.multiple_of(i * block, block), block), pl.ds(pl.multiple_of(f + i * block, block), block)
        re, im = coup[0, upper], coup[1, upper]
        b_ref[0, upper] = re
        b_ref[0, lower] = -im
        b_ref[1, upper] = im
        b_ref[1, lower] = re
        return carry

    lax.fori_loop(0, 4, couple_rows, 0)
    for b in range(lines):
        alive = jnp.concatenate([live[b]] * (f // live.shape[2]), axis=1) > 0.5
        for c in range(2):
            x = own[b % half, b // half, c].astype(F32)
            x_ref[c, b * rows : (b + 1) * rows] = jnp.where(alive, x, 0.0).astype(BF16)
    for d in range(2):
        wd[d] = window(x_ref, b_ref, d).reshape(wd.shape[1:])
    outs = [
        pltpu.make_async_copy(
            buf.at[b], out_ref.at[:, :, slot_ref[lax.bitwise_xor(me, b)]], osem.at[b]
        )
        for b in range(lines)
    ]
    total = sums_ref[...].sum(axis=0)
    cross_re, cross_im, den = total[:, :f], total[:, f : 2 * f], total[:, 2 * f :]
    wav_re, wav_im = wav_ref[0:1], wav_ref[1:2]
    scale = den + damp_ref[...]
    nw_re = wav_re + (cross_re - wav_re * den) / scale
    nw_im = wav_im + (cross_im - wav_im * den) / scale
    nw[0:1] = nw_re
    nw[1:2] = nw_im
    for b in range(lines):
        ins[b].wait()
        wg_re, wg_im = wg[0, b], wg[1, b]
        out_re = wd[0, b] - (nw_re * wg_re - nw_im * wg_im)
        out_im = wd[1, b] - (nw_re * wg_im + nw_im * wg_re)
        buf[b, 0] = out_re.reshape(shots, rb, f).astype(BF16)
        buf[b, 1] = out_im.reshape(shots, rb, f).astype(BF16)
        if b == 0:
            last = pltpu.make_async_copy(nw, nw_ref, nsem)
            last.start()
        else:
            outs[b - 1].start()
    outs[-1].start()
    for c in outs:
        c.wait()
    last.wait()


def swapped(x, axis, bit):
    size = lax.axis_size(axis)
    return lax.ppermute(x, axis, [(i, i ^ bit) for i in range(size)])


def sent_to_all(array, axis):
    size = lax.axis_size(axis)
    return lax.all_to_all(
        jnp.broadcast_to(array[None], (size, *array.shape)), axis, 0, 0, tiled=True
    )


def update(modeled, observed, mask, shot_order, line_of_slot, coupling, wavelet, damping):
    _, shots, lines, rb, f = modeled.shape
    slots = lax.axis_size(SHOT)
    held = observed.shape[2]
    pieces = lax.axis_size(RCV)
    rows = shots * rb
    traces = lines * rows
    flops = 8 * traces * f * f
    me = lax.axis_index(SHOT).astype(jnp.int32).reshape(1)

    own_spread = call(
        k_spread, jax.ShapeDtypeStruct((pieces, 2 * held, rb, f), BF16), [ANY], HBM,
        limit=BIG,
        scratch=[
            pltpu.VMEM((pieces, 2 * held, rb, f), BF16),
            pltpu.SemaphoreType.DMA((CHUNKS, 2 * held)),
            pltpu.SemaphoreType.DMA((CHUNKS,)),
        ],
    )(observed.reshape(2 * held, pieces, rb, f))
    own_natural = lax.all_to_all(own_spread, RCV, 0, 0, tiled=True)

    piece = jax.ShapeDtypeStruct((2, rows, f), BF16)
    live, *masked = call(
        k_mask, (jax.ShapeDtypeStruct((slots, rows, 128), F32), *[piece] * slots),
        [SM, SM, VM, VM],
    )(me, line_of_slot, modeled, mask)
    wide = jax.ShapeDtypeStruct((2, slots, rows, f), F32)
    dma = pltpu.SemaphoreType.DMA
    coup = pltpu.VMEM(coupling.shape, BF16)
    x_block = pltpu.VMEM((2, traces, f), BF16)
    b_block = pltpu.VMEM((2, 2 * f, f), BF16)
    w_block = pltpu.VMEM(wide.shape, F32)
    window_scratch = [coup, x_block, b_block, w_block, dma, dma((slots,)), dma((2,))]
    arrived = {0: masked[0]}
    for b in SWAPS:
        arrived[b] = swapped(masked[b], SHOT, b)
    wg_here = call(
        k_window, wide, [ANY] * (slots + 1), HBM, flops=flops,
        scratch=window_scratch, limit=WIN,
    )(*masked, coupling)
    half = slots // 2
    quad = jax.ShapeDtypeStruct((half, 2, rows, f), BF16)
    own_send, own_keep = call(
        k_group, (quad, quad), [SM, SM, VM], [HBM, VM], limit=GRP,
        scratch=[pltpu.VMEM(quad.shape, BF16), dma((half,))],
    )(
        me, shot_order, own_natural.reshape(pieces, held, 2, rb, f)
    )
    own_came = swapped(own_send, "xh", 1)
    sums = call(
        k_cross, jax.ShapeDtypeStruct((3, f), F32), [SM, SM, VM, VM] + [ANY] * slots,
        scratch=[x_block, x_block, b_block, dma((slots,))],
        limit=CRS, flops=2 * flops,
    )(me, shot_order, own_natural.reshape(pieces, held, 2, rb, f), coupling, *[arrived[b] for b in range(slots)])
    part = sent_to_all(sums.reshape(1, 3 * f), PILE).sum(axis=0)
    couple_of = jax.ShapeDtypeStruct((2, 2, rows, f), BF16)
    pairs = call(k_pair, (couple_of,) * half, [ANY, ANY], scratch=[dma((2, half))])(own_keep, own_came)
    met = {0: pairs[0]}
    for b in (1, 3, 2):
        met[b] = swapped(pairs[b], ("yh", "yl"), b)
    parts = sent_to_all(part, REST)
    new_wavelet, residual = call(
        k_final,
        (jax.ShapeDtypeStruct((2, f), F32), jax.ShapeDtypeStruct(modeled.shape, BF16)),
        [SM, SM] + [ANY] * (half + 2) + [HBM, VM, VM, VM], [HBM, HBM],
        scratch=[
            pltpu.VMEM((half, 2, 2, rows, f), BF16), pltpu.VMEM(live.shape, F32), coup, x_block, b_block,
            w_block, w_block, pltpu.VMEM((slots, 2, shots, rb, f), BF16), pltpu.VMEM((2, f), F32),
            dma((half,)), dma((2,)), dma((slots,)), dma((slots,)), dma,
        ],
        limit=FIN, flops=flops,
    )(
        me, line_of_slot, *[met[d] for d in range(half)], live, coupling, wg_here,
        parts, wavelet, damping.reshape(1, f),
    )
    return new_wavelet, residual


def solution(mesh):
    fine = Mesh(mesh.devices.reshape((2,) * 8), SHOT + RCV)
    placed = (
        P(None, SHOT, None, RCV, None),
        P(None, SHOT, RCV, None, None),
        P(SHOT, None, RCV),
        P(),
        P(),
        P(),
        P(),
        P(),
    )
    return jax.shard_map(
        update,
        mesh=fine,
        in_specs=placed,
        out_specs=(P(), P(None, SHOT, None, RCV, None)),
        check_vma=False,
    )
```

profile of v0, /device:TPU:8, one launch (start us, length us, event | category | flops | bytes accessed | tf_op | source)
XLA Modules:
  0.0 104.0 jit_solution(6746847901050755451)
XLA Ops:
  0.6 2.1 %shard_map.95 = bf16[32,4,8,512]{3,2,1,0:T(8,128)(2,1)} custom-call(bf16[4,32,8,512]{3,2,1,0:T(8,128)(2,1)} %bitcast.7), custom_call_target="tpu_custom_call" | custom-call | bytes 1048576 | tf_op jit(solution)/shard_map/pallas_call | solution.py:297
  2.8 9.9 %all-to-all-start = ((bf16[32,4,8,512]{3,2,1,0:T(8,128)(2,1)}), bf16[32,4,8,512]{3,2,1,0:T(8,128)(2,1)S(1)}, u32[]{:S(2)}, u32[]{:S(2)}) async-start(bf16[32,4,8,512]{3,2,1,0:T(8,128)(2,1)} %shard_map.95), calls=%async_computation | async-start | bytes 2097152 | tf_op jit(solution)/shard_map/all_to_all | solution.py:306
  12.7 28.5 %all-to-all-done = bf16[32,4,8,512]{3,2,1,0:T(8,128)(2,1)S(1)} async-done(((bf16[32,4,8,512]{3,2,1,0:T(8,128)(2,1)}), bf16[32,4,8,512]{3,2,1,0:T(8,128)(2,1)S(1)}, u32[]{:S(2)}, u32[]{:S(2)}) %all-to-all-start) | async-done | bytes 1048608 | tf_op jit(solution)/shard_map/all_to_all | solution.py:306
  41.2 1.4 %shard_map.96 = (bf16[4,2,64,512]{3,2,1,0:T(8,128)(2,1)}, bf16[4,2,64,512]{3,2,1,0:T(8,128)(2,1)S(1)}) custom-call(s32[1]{0:T(128)} %bitcast.me_ref, s32[64]{0:T(128)S(1)} %copy-done.17, bf16[32,2,2,8,512]{4,3,2,1,0:T(8,128)(2,1)S(1)} %bitcast.4), custom_call_target="tpu_custom_call" | custom-call | bytes 1048576 | tf_op jit(solution)/shard_map/pallas_call | solution.py:329
  42.6 2.8 %collective-permute-start = (bf16[4,2,64,512]{3,2,1,0:T(8,128)(2,1)}, bf16[4,2,64,512]{3,2,1,0:T(8,128)(2,1)}, u32[]{:S(2)}, u32[]{:S(2)}) collective-permute-start(bf16[4,2,64,512]{3,2,1,0:T(8,128)(2,1)} %get-tuple-element.18), channel_id=1, source_target_pairs={{0,128},{128,0},{1,129},{129,1},{2,130},{130,2},{3,131},{131,3},{4... | collective-permute-start | bytes 1572872 | tf_op jit(solution)/shard_map/ppermute | solution.py:277
  45.5 0.8 copy-done.13
  46.2 0.8 shard_map.98
  47.1 0.5 collective-permute-start.4
  47.6 2.6 %collective-permute-start.5 = (bf16[2,64,512]{2,1,0:T(8,128)(2,1)S(1)}, bf16[2,64,512]{2,1,0:T(8,128)(2,1)S(1)}, u32[]{:S(2)}, u32[]{:S(2)}) collective-permute-start(bf16[2,64,512]{2,1,0:T(8,128)(2,1)S(1)} %get-tuple-element.26.refs_2_), channel_id=1, source_target_pairs={{0,64},{32,96},{64,0},{96,32},{128,192},{160,224},{192,128},{224,1... | collective-permute-start | bytes 393224 | tf_op jit(solution)/shard_map/ppermute | solution.py:277
  50.2 0.4 collective-permute-start.6
  50.7 0.8 collective-permute-start.7
  51.5 1.8 %collective-permute-done.4.refs_1_ = bf16[2,64,512]{2,1,0:T(8,128)(2,1)S(1)} collective-permute-done((bf16[2,64,512]{2,1,0:T(8,128)(2,1)S(1)}, bf16[2,64,512]{2,1,0:T(8,128)(2,1)S(1)}, u32[]{:S(2)}, u32[]{:S(2)}) %collective-permute-start.4) | collective-permute-done | bytes 131104 | tf_op jit(solution)/shard_map/ppermute | solution.py:277
  53.3 2.1 %collective-permute-start.8 = (bf16[2,64,512]{2,1,0:T(8,128)(2,1)S(1)}, bf16[2,64,512]{2,1,0:T(8,128)(2,1)S(1)}, u32[]{:S(2)}, u32[]{:S(2)}) collective-permute-start(bf16[2,64,512]{2,1,0:T(8,128)(2,1)S(1)} %get-tuple-element.29.refs_5_), channel_id=1, source_target_pairs={{0,160},{32,128},{64,224},{96,192},{128,32},{160,0},{192,96},{224,... | collective-permute-start | bytes 393224 | tf_op jit(solution)/shard_map/ppermute | solution.py:277
  55.3 2.3 %collective-permute-start.9 = (bf16[2,64,512]{2,1,0:T(8,128)(2,1)S(1)}, bf16[2,64,512]{2,1,0:T(8,128)(2,1)S(1)}, u32[]{:S(2)}, u32[]{:S(2)}) collective-permute-start(bf16[2,64,512]{2,1,0:T(8,128)(2,1)S(1)} %get-tuple-element.30.refs_6_), channel_id=1, source_target_pairs={{0,192},{32,224},{64,128},{96,160},{128,64},{160,96},{192,0},{224,... | collective-permute-start | bytes 393224 | tf_op jit(solution)/shard_map/ppermute | solution.py:277
  57.6 2.7 %collective-permute-start.10 = (bf16[2,64,512]{2,1,0:T(8,128)(2,1)S(1)}, bf16[2,64,512]{2,1,0:T(8,128)(2,1)S(1)}, u32[]{:S(2)}, u32[]{:S(2)}) collective-permute-start(bf16[2,64,512]{2,1,0:T(8,128)(2,1)S(1)} %get-tuple-element.31.refs_7_), channel_id=1, source_target_pairs={{0,224},{32,192},{64,160},{96,128},{128,96},{160,64},{192,32},{224... | collective-permute-start | bytes 393224 | tf_op jit(solution)/shard_map/ppermute | solution.py:277
  60.3 1.7 %collective-permute-done.7.refs_4_ = bf16[2,64,512]{2,1,0:T(8,128)(2,1)S(1)} collective-permute-done((bf16[2,64,512]{2,1,0:T(8,128)(2,1)S(1)}, bf16[2,64,512]{2,1,0:T(8,128)(2,1)S(1)}, u32[]{:S(2)}, u32[]{:S(2)}) %collective-permute-start.7) | collective-permute-done | bytes 131104 | tf_op jit(solution)/shard_map/ppermute | solution.py:277
  62.0 2.5 %collective-permute-done.8.refs_5_ = bf16[2,64,512]{2,1,0:T(8,128)(2,1)S(1)} collective-permute-done((bf16[2,64,512]{2,1,0:T(8,128)(2,1)S(1)}, bf16[2,64,512]{2,1,0:T(8,128)(2,1)S(1)}, u32[]{:S(2)}, u32[]{:S(2)}) %collective-permute-start.8) | collective-permute-done | bytes 131104 | tf_op jit(solution)/shard_map/ppermute | solution.py:277
  64.5 4.4 %collective-permute-done.9.refs_6_ = bf16[2,64,512]{2,1,0:T(8,128)(2,1)S(1)} collective-permute-done((bf16[2,64,512]{2,1,0:T(8,128)(2,1)S(1)}, bf16[2,64,512]{2,1,0:T(8,128)(2,1)S(1)}, u32[]{:S(2)}, u32[]{:S(2)}) %collective-permute-start.9) | collective-permute-done | bytes 131104 | tf_op jit(solution)/shard_map/ppermute | solution.py:277
  68.9 0.7 collective-permute-done.10.refs_7_
  69.6 4.3 %shard_map.100 = f32[3,512]{1,0:T(4,128)S(1)} custom-call(s32[1]{0:T(128)} %bitcast.me_ref, s32[64]{0:T(128)S(1)} %copy-done.17, bf16[32,2,2,8,512]{4,3,2,1,0:T(8,128)(2,1)S(1)} %bitcast.5, bf16[2,512,512]{2,1,0:T(8,128)(2,1)S(1)} %copy-done, bf16[2,64,512]{2,1,0:T(8,128)(2,1)S(1)} %get-tuple-element.24.refs_0_, ...), custom_call_target="tpu_custom_call" | custom-call | flops 2147483648 | bytes 1048576 | tf_op jit(solution)/shard_map/pallas_call | solution.py:336
  73.9 0.7 broadcast_in_dim.14
  74.6 4.8 %all-to-all-start.1 = ((f32[16,1,1536]{2,1,0:T(1,128)}), f32[16,1,1536]{2,1,0:T(1,128)S(1)}, u32[]{:S(2)}, u32[]{:S(2)}) async-start(f32[16,1,1536]{2,1,0:T(1,128)} %broadcast_in_dim.14), calls=%async_computation.1 | async-start | bytes 196608 | tf_op jit(solution)/shard_map/all_to_all | solution.py:282
  79.4 2.0 %shard_map.97 = (bf16[2,2,64,512]{3,2,1,0:T(8,128)(2,1)S(1)}, bf16[2,2,64,512]{3,2,1,0:T(8,128)(2,1)}, bf16[2,2,64,512]{3,2,1,0:T(8,128)(2,1)}, bf16[2,2,64,512]{3,2,1,0:T(8,128)(2,1)S(1)}) custom-call(bf16[4,2,64,512]{3,2,1,0:T(8,128)(2,1)S(1)} %copy-done.4, bf16[4,2,64,512]{3,2,1,0:T(8,128)(2,1)} %collective-permute-done.came_ref), custom_call_target="tpu_custom_call" | custom-call | bytes 1048576 | tf_op jit(solution)/shard_map/pallas_call | solution.py:343
  81.4 1.4 %collective-permute-start.1 = (bf16[2,2,64,512]{3,2,1,0:T(8,128)(2,1)}, bf16[2,2,64,512]{3,2,1,0:T(8,128)(2,1)S(1)}, u32[]{:S(2)}, u32[]{:S(2)}) collective-permute-start(bf16[2,2,64,512]{3,2,1,0:T(8,128)(2,1)} %get-tuple-element.20), channel_id=1, source_target_pairs={{0,32},{32,0},{64,96},{96,64},{1,33},{33,1},{65,97},{97,65},{2,34}... | collective-permute-start | bytes 786440 | tf_op jit(solution)/shard_map/ppermute | solution.py:277
  82.8 2.1 %collective-permute-start.3 = (bf16[2,2,64,512]{3,2,1,0:T(8,128)(2,1)S(1)}, bf16[2,2,64,512]{3,2,1,0:T(8,128)(2,1)S(1)}, u32[]{:S(2)}, u32[]{:S(2)}) collective-permute-start(bf16[2,2,64,512]{3,2,1,0:T(8,128)(2,1)S(1)} %get-tuple-element.22), channel_id=1, source_target_pairs={{0,96},{32,64},{64,32},{96,0},{1,97},{33,65},{65,33},{97,1},{2,98}... | collective-permute-start | bytes 786440 | tf_op jit(solution)/shard_map/ppermute | solution.py:277
  84.9 2.7 %all-to-all-done.1 = f32[16,1,1536]{2,1,0:T(1,128)S(1)} async-done(((f32[16,1,1536]{2,1,0:T(1,128)}), f32[16,1,1536]{2,1,0:T(1,128)S(1)}, u32[]{:S(2)}, u32[]{:S(2)}) %all-to-all-start.1) | async-done | bytes 98336 | tf_op jit(solution)/shard_map/all_to_all | solution.py:282
  87.7 0.1 reduce_sum.9
  87.8 0.7 broadcast_in_dim.15
  88.4 5.9 %all-to-all-start.2 = ((f32[16,1,1536]{2,1,0:T(1,128)}), f32[16,1,1536]{2,1,0:T(1,128)S(1)}, u32[]{:S(2)}, u32[]{:S(2)}) async-start(f32[16,1,1536]{2,1,0:T(1,128)} %broadcast_in_dim.15), calls=%async_computation.2 | async-start | bytes 196608 | tf_op jit(solution)/shard_map/all_to_all | solution.py:282
  94.3 4.4 %shard_map.99.refs_6_ = f32[2,8,64,512]{3,2,1,0:T(8,128)} custom-call(bf16[2,64,512]{2,1,0:T(8,128)(2,1)} %copy-done.5, bf16[2,64,512]{2,1,0:T(8,128)(2,1)} %copy-done.6, bf16[2,64,512]{2,1,0:T(8,128)(2,1)} %copy-done.7, bf16[2,64,512]{2,1,0:T(8,128)(2,1)} %copy-done.8, bf16[2,64,512]{2,1,0:T(8,128)(2,1)} %copy-done.9, bf16[2,64,512]{2,1,0:T(8,128)(2,1)} %copy-done.10, ...), custom_call_target="tpu_custom_call" | custom-call | flops 1073741824 | bytes 1048576 | tf_op jit(solution)/shard_map/pallas_call | solution.py:323
  98.8 1.8 %all-to-all-done.2.refs_7_ = f32[16,1,1536]{2,1,0:T(1,128)S(1)} async-done(((f32[16,1,1536]{2,1,0:T(1,128)}), f32[16,1,1536]{2,1,0:T(1,128)S(1)}, u32[]{:S(2)}, u32[]{:S(2)}) %all-to-all-start.2) | async-done | bytes 98336 | tf_op jit(solution)/shard_map/all_to_all | solution.py:282
  100.6 3.4 %shard_map.101 = (f32[2,512]{1,0:T(2,128)}, bf16[2,8,8,8,512]{4,3,2,1,0:T(8,128)(2,1)}) custom-call(s32[1]{0:T(128)} %bitcast.me_ref, s32[8]{0:T(128)S(1)} %copy-done.16, bf16[2,2,64,512]{3,2,1,0:T(8,128)(2,1)S(1)} %get-tuple-element.19.refs_0_, bf16[2,2,64,512]{3,2,1,0:T(8,128)(2,1)S(1)} %collective-permute-done.1.refs_1_, ...), custom_call_target="tpu_custom_call" | custom-call | flops 1073741824 | bytes 1048576 | tf_op jit(solution)/shard_map/pallas_call | solution.py:348
  (43 shorter events, 0.1 us)
Async XLA Ops:
  0.6 40.6 %copy-start.17 = (s32[64]{0:T(128)S(1)}, s32[64]{0:T(128)}, u32[]{:S(2)}) copy-start(s32[64]{0:T(128)} %order_ref.3) | copy-start | bytes 772
  2.8 42.7 %copy-start.2 = (bf16[2,8,8,8,512]{4,3,2,1,0:T(8,128)(2,1)S(1)}, bf16[2,8,8,8,512]{4,3,2,1,0:T(8,128)(2,1)}, u32[]{:S(2)}) copy-start(bf16[2,8,8,8,512]{4,3,2,1,0:T(8,128)(2,1)} %mod_ref.1) | copy-start | bytes 3145732
  2.8 42.7 %copy-start.16 = (s32[8]{0:T(128)S(1)}, s32[8]{0:T(128)}, u32[]{:S(2)}) copy-start(s32[8]{0:T(128)} %slot_ref.3) | copy-start | bytes 100
  2.8 66.8 %copy-start = (bf16[2,512,512]{2,1,0:T(8,128)(2,1)S(1)}, bf16[2,512,512]{2,1,0:T(8,128)(2,1)}, u32[]{:S(2)}) copy-start(bf16[2,512,512]{2,1,0:T(8,128)(2,1)} %refs_5_.1) | copy-start | bytes 3145732
  2.8 38.4 %all-to-all-start = ((bf16[32,4,8,512]{3,2,1,0:T(8,128)(2,1)}), bf16[32,4,8,512]{3,2,1,0:T(8,128)(2,1)S(1)}, u32[]{:S(2)}, u32[]{:S(2)}) async-start(bf16[32,4,8,512]{3,2,1,0:T(8,128)(2,1)} %shard_map.95), calls=%async_computation | async-start | bytes 2097152 | tf_op jit(solution)/shard_map/all_to_all | solution.py:306
  42.6 4.4 %copy-start.3 = (bf16[4,2,64,512]{3,2,1,0:T(8,128)(2,1)}, bf16[4,2,64,512]{3,2,1,0:T(8,128)(2,1)S(1)}, u32[]{:S(2)}) copy-start(bf16[4,2,64,512]{3,2,1,0:T(8,128)(2,1)S(1)} %get-tuple-element.17.keep_ref) | copy-start | bytes 1572868
  42.6 36.7 %collective-permute-start = (bf16[4,2,64,512]{3,2,1,0:T(8,128)(2,1)}, bf16[4,2,64,512]{3,2,1,0:T(8,128)(2,1)}, u32[]{:S(2)}, u32[]{:S(2)}) collective-permute-start(bf16[4,2,64,512]{3,2,1,0:T(8,128)(2,1)} %get-tuple-element.18), channel_id=1, source_target_pairs={{0,128},{128,0},{1,129},{129,1},{2,130},{130,2},{3,131},{131,3},{4... | collective-permute-start | bytes 1572872 | tf_op jit(solution)/shard_map/ppermute | solution.py:277
  45.5 0.8 copy-start.13
  47.0 22.5 %copy-start.6 = (bf16[2,64,512]{2,1,0:T(8,128)(2,1)}, bf16[2,64,512]{2,1,0:T(8,128)(2,1)S(1)}, u32[]{:S(2)}) copy-start(bf16[2,64,512]{2,1,0:T(8,128)(2,1)S(1)} %get-tuple-element.25.refs_1_) | copy-start | bytes 393220
  47.0 22.5 %copy-start.7 = (bf16[2,64,512]{2,1,0:T(8,128)(2,1)}, bf16[2,64,512]{2,1,0:T(8,128)(2,1)S(1)}, u32[]{:S(2)}) copy-start(bf16[2,64,512]{2,1,0:T(8,128)(2,1)S(1)} %get-tuple-element.26.refs_2_) | copy-start | bytes 393220
  47.1 22.5 %copy-start.8 = (bf16[2,64,512]{2,1,0:T(8,128)(2,1)}, bf16[2,64,512]{2,1,0:T(8,128)(2,1)S(1)}, u32[]{:S(2)}) copy-start(bf16[2,64,512]{2,1,0:T(8,128)(2,1)S(1)} %get-tuple-element.27.refs_3_) | copy-start | bytes 393220
  47.1 22.5 %copy-start.9 = (bf16[2,64,512]{2,1,0:T(8,128)(2,1)}, bf16[2,64,512]{2,1,0:T(8,128)(2,1)S(1)}, u32[]{:S(2)}) copy-start(bf16[2,64,512]{2,1,0:T(8,128)(2,1)S(1)} %get-tuple-element.28.refs_4_) | copy-start | bytes 393220
  47.1 22.5 %copy-start.10 = (bf16[2,64,512]{2,1,0:T(8,128)(2,1)}, bf16[2,64,512]{2,1,0:T(8,128)(2,1)S(1)}, u32[]{:S(2)}) copy-start(bf16[2,64,512]{2,1,0:T(8,128)(2,1)S(1)} %get-tuple-element.29.refs_5_) | copy-start | bytes 393220
  47.1 22.5 %copy-start.11 = (bf16[2,64,512]{2,1,0:T(8,128)(2,1)}, bf16[2,64,512]{2,1,0:T(8,128)(2,1)S(1)}, u32[]{:S(2)}) copy-start(bf16[2,64,512]{2,1,0:T(8,128)(2,1)S(1)} %get-tuple-element.30.refs_6_) | copy-start | bytes 393220
  47.1 22.5 %copy-start.12 = (bf16[2,64,512]{2,1,0:T(8,128)(2,1)}, bf16[2,64,512]{2,1,0:T(8,128)(2,1)S(1)}, u32[]{:S(2)}) copy-start(bf16[2,64,512]{2,1,0:T(8,128)(2,1)S(1)} %get-tuple-element.31.refs_7_) | copy-start | bytes 393220
  47.1 26.8 %copy-start.5 = (bf16[2,64,512]{2,1,0:T(8,128)(2,1)}, bf16[2,64,512]{2,1,0:T(8,128)(2,1)S(1)}, u32[]{:S(2)}) copy-start(bf16[2,64,512]{2,1,0:T(8,128)(2,1)S(1)} %get-tuple-element.24.refs_0_) | copy-start | bytes 393220
  47.1 6.1 %collective-permute-start.4 = (bf16[2,64,512]{2,1,0:T(8,128)(2,1)S(1)}, bf16[2,64,512]{2,1,0:T(8,128)(2,1)S(1)}, u32[]{:S(2)}, u32[]{:S(2)}) collective-permute-start(bf16[2,64,512]{2,1,0:T(8,128)(2,1)S(1)} %get-tuple-element.25.refs_1_), channel_id=1, source_target_pairs={{0,32},{32,0},{64,96},{96,64},{128,160},{160,128},{192,224},{224,1... | collective-permute-start | bytes 393224 | tf_op jit(solution)/shard_map/ppermute | solution.py:277
  47.6 7.7 %collective-permute-start.5 = (bf16[2,64,512]{2,1,0:T(8,128)(2,1)S(1)}, bf16[2,64,512]{2,1,0:T(8,128)(2,1)S(1)}, u32[]{:S(2)}, u32[]{:S(2)}) collective-permute-start(bf16[2,64,512]{2,1,0:T(8,128)(2,1)S(1)} %get-tuple-element.26.refs_2_), channel_id=1, source_target_pairs={{0,64},{32,96},{64,0},{96,32},{128,192},{160,224},{192,128},{224,1... | collective-permute-start | bytes 393224 | tf_op jit(solution)/shard_map/ppermute | solution.py:277
  50.2 7.4 %collective-permute-start.6 = (bf16[2,64,512]{2,1,0:T(8,128)(2,1)S(1)}, bf16[2,64,512]{2,1,0:T(8,128)(2,1)S(1)}, u32[]{:S(2)}, u32[]{:S(2)}) collective-permute-start(bf16[2,64,512]{2,1,0:T(8,128)(2,1)S(1)} %get-tuple-element.27.refs_3_), channel_id=1, source_target_pairs={{0,96},{32,64},{64,32},{96,0},{128,224},{160,192},{192,160},{224,1... | collective-permute-start | bytes 393224 | tf_op jit(solution)/shard_map/ppermute | solution.py:277
  50.7 11.4 %collective-permute-start.7 = (bf16[2,64,512]{2,1,0:T(8,128)(2,1)S(1)}, bf16[2,64,512]{2,1,0:T(8,128)(2,1)S(1)}, u32[]{:S(2)}, u32[]{:S(2)}) collective-permute-start(bf16[2,64,512]{2,1,0:T(8,128)(2,1)S(1)} %get-tuple-element.28.refs_4_), channel_id=1, source_target_pairs={{0,128},{32,160},{64,192},{96,224},{128,0},{160,32},{192,64},{224,... | collective-permute-start | bytes 393224 | tf_op jit(solution)/shard_map/ppermute | solution.py:277
  53.3 11.2 %collective-permute-start.8 = (bf16[2,64,512]{2,1,0:T(8,128)(2,1)S(1)}, bf16[2,64,512]{2,1,0:T(8,128)(2,1)S(1)}, u32[]{:S(2)}, u32[]{:S(2)}) collective-permute-start(bf16[2,64,512]{2,1,0:T(8,128)(2,1)S(1)} %get-tuple-element.29.refs_5_), channel_id=1, source_target_pairs={{0,160},{32,128},{64,224},{96,192},{128,32},{160,0},{192,96},{224,... | collective-permute-start | bytes 393224 | tf_op jit(solution)/shard_map/ppermute | solution.py:277
  55.3 13.5 %collective-permute-start.9 = (bf16[2,64,512]{2,1,0:T(8,128)(2,1)S(1)}, bf16[2,64,512]{2,1,0:T(8,128)(2,1)S(1)}, u32[]{:S(2)}, u32[]{:S(2)}) collective-permute-start(bf16[2,64,512]{2,1,0:T(8,128)(2,1)S(1)} %get-tuple-element.30.refs_6_), channel_id=1, source_target_pairs={{0,192},{32,224},{64,128},{96,160},{128,64},{160,96},{192,0},{224,... | collective-permute-start | bytes 393224 | tf_op jit(solution)/shard_map/ppermute | solution.py:277
  57.6 11.9 %collective-permute-start.10 = (bf16[2,64,512]{2,1,0:T(8,128)(2,1)S(1)}, bf16[2,64,512]{2,1,0:T(8,128)(2,1)S(1)}, u32[]{:S(2)}, u32[]{:S(2)}) collective-permute-start(bf16[2,64,512]{2,1,0:T(8,128)(2,1)S(1)} %get-tuple-element.31.refs_7_), channel_id=1, source_target_pairs={{0,224},{32,192},{64,160},{96,128},{128,96},{160,64},{192,32},{224... | collective-permute-start | bytes 393224 | tf_op jit(solution)/shard_map/ppermute | solution.py:277
  69.6 9.8 %copy-start.4 = (bf16[4,2,64,512]{3,2,1,0:T(8,128)(2,1)S(1)}, bf16[4,2,64,512]{3,2,1,0:T(8,128)(2,1)}, u32[]{:S(2)}) copy-start(bf16[4,2,64,512]{3,2,1,0:T(8,128)(2,1)} %copy-done.3) | copy-start | bytes 1572868
  74.6 13.1 %all-to-all-start.1 = ((f32[16,1,1536]{2,1,0:T(1,128)}), f32[16,1,1536]{2,1,0:T(1,128)S(1)}, u32[]{:S(2)}, u32[]{:S(2)}) async-start(f32[16,1,1536]{2,1,0:T(1,128)} %broadcast_in_dim.14), calls=%async_computation.1 | async-start | bytes 196608 | tf_op jit(solution)/shard_map/all_to_all | solution.py:282
  81.4 19.2 %collective-permute-start.1 = (bf16[2,2,64,512]{3,2,1,0:T(8,128)(2,1)}, bf16[2,2,64,512]{3,2,1,0:T(8,128)(2,1)S(1)}, u32[]{:S(2)}, u32[]{:S(2)}) collective-permute-start(bf16[2,2,64,512]{3,2,1,0:T(8,128)(2,1)} %get-tuple-element.20), channel_id=1, source_target_pairs={{0,32},{32,0},{64,96},{96,64},{1,33},{33,1},{65,97},{97,65},{2,34}... | collective-permute-start | bytes 786440 | tf_op jit(solution)/shard_map/ppermute | solution.py:277
  82.8 17.8 %collective-permute-start.2 = (bf16[2,2,64,512]{3,2,1,0:T(8,128)(2,1)}, bf16[2,2,64,512]{3,2,1,0:T(8,128)(2,1)S(1)}, u32[]{:S(2)}, u32[]{:S(2)}) collective-permute-start(bf16[2,2,64,512]{3,2,1,0:T(8,128)(2,1)} %get-tuple-element.21), channel_id=1, source_target_pairs={{0,64},{32,96},{64,0},{96,32},{1,65},{33,97},{65,1},{97,33},{2,66}... | collective-permute-start | bytes 786440 | tf_op jit(solution)/shard_map/ppermute | solution.py:277
  82.8 17.8 %collective-permute-start.3 = (bf16[2,2,64,512]{3,2,1,0:T(8,128)(2,1)S(1)}, bf16[2,2,64,512]{3,2,1,0:T(8,128)(2,1)S(1)}, u32[]{:S(2)}, u32[]{:S(2)}) collective-permute-start(bf16[2,2,64,512]{3,2,1,0:T(8,128)(2,1)S(1)} %get-tuple-element.22), channel_id=1, source_target_pairs={{0,96},{32,64},{64,32},{96,0},{1,97},{33,65},{65,33},{97,1},{2,98}... | collective-permute-start | bytes 786440 | tf_op jit(solution)/shard_map/ppermute | solution.py:277
  88.4 12.1 %all-to-all-start.2 = ((f32[16,1,1536]{2,1,0:T(1,128)}), f32[16,1,1536]{2,1,0:T(1,128)S(1)}, u32[]{:S(2)}, u32[]{:S(2)}) async-start(f32[16,1,1536]{2,1,0:T(1,128)} %broadcast_in_dim.15), calls=%async_computation.2 | async-start | bytes 196608 | tf_op jit(solution)/shard_map/all_to_all | solution.py:282
  94.3 6.3 %copy-start.1 = (bf16[2,512,512]{2,1,0:T(8,128)(2,1)S(1)}, bf16[2,512,512]{2,1,0:T(8,128)(2,1)}, u32[]{:S(2)}) copy-start(bf16[2,512,512]{2,1,0:T(8,128)(2,1)} %refs_5_.1) | copy-start | bytes 3145732
  94.3 6.3 %copy-start.14 = (f32[2,512]{1,0:T(2,128)S(1)}, f32[2,512]{1,0:T(2,128)}, u32[]{:S(2)}) copy-start(f32[2,512]{1,0:T(2,128)} %refs_8_.3) | copy-start | bytes 12292
  94.3 6.3 %copy-start.15 = (f32[512]{0:T(512)S(1)}, f32[512]{0:T(512)}, u32[]{:S(2)}) copy-start(f32[512]{0:T(512)} %param.15) | copy-start | bytes 6148
where the time goes:
time: 106 us; the launch traced here: 104 us
  waiting for transfers between devices  44 us (42%)
  starting transfers between devices  38.4 us (36%)
  Pallas kernels  18.4 us (17%)
  local copies, waits for them, and re-layouts  2.23 us (2%)
    all_to_all x1, waiting for transfers between devices, update(): own_natural = lax.all_to_all(own_spread, RCV, 0, 0, tiled=True)  28.5 us
    ppermute x11, starting transfers between devices, swapped(): return lax.ppermute(x, axis, [(i, i ^ bit) for i in range(size)])  17.8 us
    ppermute x11, waiting for transfers between devices, swapped(): return lax.ppermute(x, axis, [(i, i ^ bit) for i in range(size)])  11 us
    all_to_all x2, starting transfers between devices, sent_to_all(): lax.all_to_all(jnp.broadcast_to(array[None], (size, *array.shape)), axis,...  10.6 us
    all_to_all x1, starting transfers between devices, update(): own_natural = lax.all_to_all(own_spread, RCV, 0, 0, tiled=True)  9.92 us
    all_to_all x2, waiting for transfers between devices, sent_to_all(): lax.all_to_all(jnp.broadcast_to(array[None], (size, *array.shape)), axis,...  4.55 us
    pallas_call x1, Pallas kernels, update(): call(k_window, wide, [ANY] * (slots + 1), HBM, flops=flops, scratch=windo...  4.45 us
    pallas_call x1, Pallas kernels, update(): call(k_cross, jax.ShapeDtypeStruct((3, f), F32), [SM, SM, VM, VM] + [ANY]...  4.26 us
  transfers between devices with their start and end apart: 14, of which 8 were waited for; matrix products, arithmetic and copies ran while one was open for 1% of the time, Pallas kernels for 11%

commit v1 on v0

--- a/solution.py
+++ b/solution.py
@@ -127,13 +127,12 @@
     return x.reshape(x.shape[0] // 8, 8, x.shape[1]).sum(axis=0).sum(axis=0, keepdims=True)
 
 
-def k_group(me_ref, order_ref, own_ref, send_ref, keep_ref, buf, sem):
+def k_group(me_ref, order_ref, own_ref, send_ref, keep_ref):
     me = me_ref[0]
     half, _, rows, _ = send_ref.shape
     rb = own_ref.shape[3]
     size = rows // rb
-    copies = [pltpu.make_async_copy(buf.at[d], send_ref.at[d], sem.at[d]) for d in range(half)]
-    for first, to in ((half, buf), (0, keep_ref)):
+    for first, out_ref in ((half, send_ref), (0, keep_ref)):
         for d in range(half):
             g = lax.bitwise_xor(me, first + d)
             for s in range(size):
@@ -141,26 +140,13 @@
                 j = lax.shift_right_logical(n, 1)
                 h = lax.bitwise_and(n, 1)
                 for c in range(2):
-                    to[d, c, s * rb : (s + 1) * rb] = own_ref[j, h, c]
-            if first and d:
-                copies[d - 1].start()
-        if first:
-            copies[-1].start()
-    for c in copies:
-        c.wait()
-
-
-def k_pair(keep_ref, came_ref, *refs):
-    out_refs, sem = refs[:-1], refs[-1]
-    copies = [
-        pltpu.make_async_copy(src.at[d], out_ref.at[i], sem.at[i, d])
-        for i, src in ((1, came_ref), (0, keep_ref))
-        for d, out_ref in enumerate(out_refs)
-    ]
-    for c in copies:
-        c.start()
-    for c in copies:
-        c.wait()
+                    out_ref[d, c, s * rb : (s + 1) * rb] = own_ref[j, h, c]
+
+
+def k_pair(keep_ref, came_ref, *out_refs):
+    for d, out_ref in enumerate(out_refs):
+        out_ref[0] = keep_ref[d]
+        out_ref[1] = came_ref[d]
 
 
 def k_cross(me_ref, order_ref, own_ref, c_ref, *refs):
@@ -326,10 +312,7 @@
     )(*masked, coupling)
     half = slots // 2
     quad = jax.ShapeDtypeStruct((half, 2, rows, f), BF16)
-    own_send, own_keep = call(
-        k_group, (quad, quad), [SM, SM, VM], [HBM, VM], limit=GRP,
-        scratch=[pltpu.VMEM(quad.shape, BF16), dma((half,))],
-    )(
+    own_send, own_keep = call(k_group, (quad, quad), [SM, SM, VM], limit=GRP)(
         me, shot_order, own_natural.reshape(pieces, held, 2, rb, f)
     )
     own_came = swapped(own_send, "xh", 1)
@@ -340,9 +323,9 @@
     )(me, shot_order, own_natural.reshape(pieces, held, 2, rb, f), coupling, *[arrived[b] for b in range(slots)])
     part = sent_to_all(sums.reshape(1, 3 * f), PILE).sum(axis=0)
     couple_of = jax.ShapeDtypeStruct((2, 2, rows, f), BF16)
-    pairs = call(k_pair, (couple_of,) * half, [ANY, ANY], scratch=[dma((2, half))])(own_keep, own_came)
+    pairs = call(k_pair, (couple_of,) * half, [VM, VM])(own_keep, own_came)
     met = {0: pairs[0]}
-    for b in (1, 3, 2):
+    for b in (2, 1, 3):
         met[b] = swapped(pairs[b], ("yh", "yl"), b)
     parts = sent_to_all(part, REST)
     new_wavelet, residual = call(

time: 106 us -> 106 us (level)
  no operation moved by 1% of the time
where the time goes in v1:
time: 106 us; the launch traced here: 104 us
  waiting for transfers between devices  44.2 us (42%)
  starting transfers between devices  38.2 us (36%)
  Pallas kernels  18.4 us (17%)
  local copies, waits for them, and re-layouts  2.23 us (2%)
    all_to_all x1, waiting for transfers between devices, update(): own_natural = lax.all_to_all(own_spread, RCV, 0, 0, tiled=True)  28.5 us
    ppermute x11, starting transfers between devices, swapped(): return lax.ppermute(x, axis, [(i, i ^ bit) for i in range(size)])  17.7 us
    ppermute x11, waiting for transfers between devices, swapped(): return lax.ppermute(x, axis, [(i, i ^ bit) for i in range(size)])  11 us
    all_to_all x2, starting transfers between devices, sent_to_all(): lax.all_to_all(jnp.broadcast_to(array[None], (size, *array.shape)), axis,...  10.6 us
    all_to_all x1, starting transfers between devices, update(): own_natural = lax.all_to_all(own_spread, RCV, 0, 0, tiled=True)  9.92 us
    all_to_all x2, waiting for transfers between devices, sent_to_all(): lax.all_to_all(jnp.broadcast_to(array[None], (size, *array.shape)), axis,...  4.74 us
    pallas_call x1, Pallas kernels, update(): call(k_window, wide, [ANY] * (slots + 1), HBM, flops=flops, scratch=windo...  4.45 us
    pallas_call x1, Pallas kernels, update(): call(k_cross, jax.ShapeDtypeStruct((3, f), F32), [SM, SM, VM, VM] + [ANY]...  4.26 us
  transfers between devices with their start and end apart: 14, of which 8 were waited for; matrix products, arithmetic and copies ran while one was open for 1% of the time, Pallas kernels for 11%

profile of v1, /device:TPU:8, one launch (start us, length us, event | category | flops | bytes accessed | tf_op | source)
XLA Modules:
  0.0 104.0 jit_solution(2772636348411792775)
XLA Ops:
  0.6 2.1 %shard_map.95 = bf16[32,4,8,512]{3,2,1,0:T(8,128)(2,1)} custom-call(bf16[4,32,8,512]{3,2,1,0:T(8,128)(2,1)} %bitcast.7), custom_call_target="tpu_custom_call" | custom-call | bytes 1048576 | tf_op jit(solution)/shard_map/pallas_call | solution.py:283
  2.8 9.9 %all-to-all-start = ((bf16[32,4,8,512]{3,2,1,0:T(8,128)(2,1)}), bf16[32,4,8,512]{3,2,1,0:T(8,128)(2,1)S(1)}, u32[]{:S(2)}, u32[]{:S(2)}) async-start(bf16[32,4,8,512]{3,2,1,0:T(8,128)(2,1)} %shard_map.95), calls=%async_computation | async-start | bytes 2097152 | tf_op jit(solution)/shard_map/all_to_all | solution.py:292
  12.7 28.5 %all-to-all-done = bf16[32,4,8,512]{3,2,1,0:T(8,128)(2,1)S(1)} async-done(((bf16[32,4,8,512]{3,2,1,0:T(8,128)(2,1)}), bf16[32,4,8,512]{3,2,1,0:T(8,128)(2,1)S(1)}, u32[]{:S(2)}, u32[]{:S(2)}) %all-to-all-start) | async-done | bytes 1048608 | tf_op jit(solution)/shard_map/all_to_all | solution.py:292
  41.2 1.5 %shard_map.96 = (bf16[4,2,64,512]{3,2,1,0:T(8,128)(2,1)}, bf16[4,2,64,512]{3,2,1,0:T(8,128)(2,1)S(1)}) custom-call(s32[1]{0:T(128)} %bitcast.me_ref, s32[64]{0:T(128)S(1)} %copy-done.17, bf16[32,2,2,8,512]{4,3,2,1,0:T(8,128)(2,1)S(1)} %bitcast.4), custom_call_target="tpu_custom_call" | custom-call | bytes 1048576 | tf_op jit(solution)/shard_map/pallas_call | solution.py:315
  42.7 2.7 %collective-permute-start = (bf16[4,2,64,512]{3,2,1,0:T(8,128)(2,1)}, bf16[4,2,64,512]{3,2,1,0:T(8,128)(2,1)}, u32[]{:S(2)}, u32[]{:S(2)}) collective-permute-start(bf16[4,2,64,512]{3,2,1,0:T(8,128)(2,1)} %get-tuple-element.18), channel_id=1, source_target_pairs={{0,128},{128,0},{1,129},{129,1},{2,130},{130,2},{3,131},{131,3},{4... | collective-permute-start | bytes 1572872 | tf_op jit(solution)/shard_map/ppermute | solution.py:263
  45.5 0.8 copy-done.13
  46.2 0.8 shard_map.98
  47.1 0.5 collective-permute-start.4
  47.6 2.6 %collective-permute-start.5 = (bf16[2,64,512]{2,1,0:T(8,128)(2,1)S(1)}, bf16[2,64,512]{2,1,0:T(8,128)(2,1)S(1)}, u32[]{:S(2)}, u32[]{:S(2)}) collective-permute-start(bf16[2,64,512]{2,1,0:T(8,128)(2,1)S(1)} %get-tuple-element.26.refs_2_), channel_id=1, source_target_pairs={{0,64},{32,96},{64,0},{96,32},{128,192},{160,224},{192,128},{224,1... | collective-permute-start | bytes 393224 | tf_op jit(solution)/shard_map/ppermute | solution.py:263
  50.2 0.4 collective-permute-start.6
  50.7 0.8 collective-permute-start.7
  51.5 1.8 %collective-permute-done.4.refs_1_ = bf16[2,64,512]{2,1,0:T(8,128)(2,1)S(1)} collective-permute-done((bf16[2,64,512]{2,1,0:T(8,128)(2,1)S(1)}, bf16[2,64,512]{2,1,0:T(8,128)(2,1)S(1)}, u32[]{:S(2)}, u32[]{:S(2)}) %collective-permute-start.4) | collective-permute-done | bytes 131104 | tf_op jit(solution)/shard_map/ppermute | solution.py:263
  53.3 2.1 %collective-permute-start.8 = (bf16[2,64,512]{2,1,0:T(8,128)(2,1)S(1)}, bf16[2,64,512]{2,1,0:T(8,128)(2,1)S(1)}, u32[]{:S(2)}, u32[]{:S(2)}) collective-permute-start(bf16[2,64,512]{2,1,0:T(8,128)(2,1)S(1)} %get-tuple-element.29.refs_5_), channel_id=1, source_target_pairs={{0,160},{32,128},{64,224},{96,192},{128,32},{160,0},{192,96},{224,... | collective-permute-start | bytes 393224 | tf_op jit(solution)/shard_map/ppermute | solution.py:263
  55.3 2.3 %collective-permute-start.9 = (bf16[2,64,512]{2,1,0:T(8,128)(2,1)S(1)}, bf16[2,64,512]{2,1,0:T(8,128)(2,1)S(1)}, u32[]{:S(2)}, u32[]{:S(2)}) collective-permute-start(bf16[2,64,512]{2,1,0:T(8,128)(2,1)S(1)} %get-tuple-element.30.refs_6_), channel_id=1, source_target_pairs={{0,192},{32,224},{64,128},{96,160},{128,64},{160,96},{192,0},{224,... | collective-permute-start | bytes 393224 | tf_op jit(solution)/shard_map/ppermute | solution.py:263
  57.6 2.7 %collective-permute-start.10 = (bf16[2,64,512]{2,1,0:T(8,128)(2,1)S(1)}, bf16[2,64,512]{2,1,0:T(8,128)(2,1)S(1)}, u32[]{:S(2)}, u32[]{:S(2)}) collective-permute-start(bf16[2,64,512]{2,1,0:T(8,128)(2,1)S(1)} %get-tuple-element.31.refs_7_), channel_id=1, source_target_pairs={{0,224},{32,192},{64,160},{96,128},{128,96},{160,64},{192,32},{224... | collective-permute-start | bytes 393224 | tf_op jit(solution)/shard_map/ppermute | solution.py:263
  60.3 1.7 %collective-permute-done.7.refs_4_ = bf16[2,64,512]{2,1,0:T(8,128)(2,1)S(1)} collective-permute-done((bf16[2,64,512]{2,1,0:T(8,128)(2,1)S(1)}, bf16[2,64,512]{2,1,0:T(8,128)(2,1)S(1)}, u32[]{:S(2)}, u32[]{:S(2)}) %collective-permute-start.7) | collective-permute-done | bytes 131104 | tf_op jit(solution)/shard_map/ppermute | solution.py:263
  62.0 2.5 %collective-permute-done.8.refs_5_ = bf16[2,64,512]{2,1,0:T(8,128)(2,1)S(1)} collective-permute-done((bf16[2,64,512]{2,1,0:T(8,128)(2,1)S(1)}, bf16[2,64,512]{2,1,0:T(8,128)(2,1)S(1)}, u32[]{:S(2)}, u32[]{:S(2)}) %collective-permute-start.8) | collective-permute-done | bytes 131104 | tf_op jit(solution)/shard_map/ppermute | solution.py:263
  64.5 4.4 %collective-permute-done.9.refs_6_ = bf16[2,64,512]{2,1,0:T(8,128)(2,1)S(1)} collective-permute-done((bf16[2,64,512]{2,1,0:T(8,128)(2,1)S(1)}, bf16[2,64,512]{2,1,0:T(8,128)(2,1)S(1)}, u32[]{:S(2)}, u32[]{:S(2)}) %collective-permute-start.9) | collective-permute-done | bytes 131104 | tf_op jit(solution)/shard_map/ppermute | solution.py:263
  68.9 0.7 collective-permute-done.10.refs_7_
  69.6 4.3 %shard_map.100 = f32[3,512]{1,0:T(4,128)S(1)} custom-call(s32[1]{0:T(128)} %bitcast.me_ref, s32[64]{0:T(128)S(1)} %copy-done.17, bf16[32,2,2,8,512]{4,3,2,1,0:T(8,128)(2,1)S(1)} %bitcast.5, bf16[2,512,512]{2,1,0:T(8,128)(2,1)S(1)} %copy-done, bf16[2,64,512]{2,1,0:T(8,128)(2,1)S(1)} %get-tuple-element.24.refs_0_, ...), custom_call_target="tpu_custom_call" | custom-call | flops 2147483648 | bytes 1048576 | tf_op jit(solution)/shard_map/pallas_call | solution.py:319
  73.9 0.7 broadcast_in_dim.14
  74.6 4.8 %all-to-all-start.1 = ((f32[16,1,1536]{2,1,0:T(1,128)}), f32[16,1,1536]{2,1,0:T(1,128)S(1)}, u32[]{:S(2)}, u32[]{:S(2)}) async-start(f32[16,1,1536]{2,1,0:T(1,128)} %broadcast_in_dim.14), calls=%async_computation.1 | async-start | bytes 196608 | tf_op jit(solution)/shard_map/all_to_all | solution.py:268
  79.4 1.9 %shard_map.97 = (bf16[2,2,64,512]{3,2,1,0:T(8,128)(2,1)S(1)}, bf16[2,2,64,512]{3,2,1,0:T(8,128)(2,1)}, bf16[2,2,64,512]{3,2,1,0:T(8,128)(2,1)}, bf16[2,2,64,512]{3,2,1,0:T(8,128)(2,1)S(1)}) custom-call(bf16[4,2,64,512]{3,2,1,0:T(8,128)(2,1)S(1)} %copy-done.4, bf16[4,2,64,512]{3,2,1,0:T(8,128)(2,1)} %collective-permute-done.came_ref), custom_call_target="tpu_custom_call" | custom-call | bytes 1048576 | tf_op jit(solution)/shard_map/pallas_call | solution.py:326
  81.2 1.3 %collective-permute-start.1 = (bf16[2,2,64,512]{3,2,1,0:T(8,128)(2,1)}, bf16[2,2,64,512]{3,2,1,0:T(8,128)(2,1)S(1)}, u32[]{:S(2)}, u32[]{:S(2)}) collective-permute-start(bf16[2,2,64,512]{3,2,1,0:T(8,128)(2,1)} %get-tuple-element.20), channel_id=1, source_target_pairs={{0,32},{32,0},{64,96},{96,64},{1,33},{33,1},{65,97},{97,65},{2,34}... | collective-permute-start | bytes 786440 | tf_op jit(solution)/shard_map/ppermute | solution.py:263
  82.6 2.1 %collective-permute-start.3 = (bf16[2,2,64,512]{3,2,1,0:T(8,128)(2,1)S(1)}, bf16[2,2,64,512]{3,2,1,0:T(8,128)(2,1)S(1)}, u32[]{:S(2)}, u32[]{:S(2)}) collective-permute-start(bf16[2,2,64,512]{3,2,1,0:T(8,128)(2,1)S(1)} %get-tuple-element.22), channel_id=1, source_target_pairs={{0,96},{32,64},{64,32},{96,0},{1,97},{33,65},{65,33},{97,1},{2,98}... | collective-permute-start | bytes 786440 | tf_op jit(solution)/shard_map/ppermute | solution.py:263
  84.7 2.9 %all-to-all-done.1 = f32[16,1,1536]{2,1,0:T(1,128)S(1)} async-done(((f32[16,1,1536]{2,1,0:T(1,128)}), f32[16,1,1536]{2,1,0:T(1,128)S(1)}, u32[]{:S(2)}, u32[]{:S(2)}) %all-to-all-start.1) | async-done | bytes 98336 | tf_op jit(solution)/shard_map/all_to_all | solution.py:268
  87.7 0.1 reduce_sum.9
  87.7 0.7 broadcast_in_dim.15
  88.4 5.9 %all-to-all-start.2 = ((f32[16,1,1536]{2,1,0:T(1,128)}), f32[16,1,1536]{2,1,0:T(1,128)S(1)}, u32[]{:S(2)}, u32[]{:S(2)}) async-start(f32[16,1,1536]{2,1,0:T(1,128)} %broadcast_in_dim.15), calls=%async_computation.2 | async-start | bytes 196608 | tf_op jit(solution)/shard_map/all_to_all | solution.py:268
  94.3 4.4 %shard_map.99.refs_6_ = f32[2,8,64,512]{3,2,1,0:T(8,128)} custom-call(bf16[2,64,512]{2,1,0:T(8,128)(2,1)} %copy-done.5, bf16[2,64,512]{2,1,0:T(8,128)(2,1)} %copy-done.6, bf16[2,64,512]{2,1,0:T(8,128)(2,1)} %copy-done.7, bf16[2,64,512]{2,1,0:T(8,128)(2,1)} %copy-done.8, bf16[2,64,512]{2,1,0:T(8,128)(2,1)} %copy-done.9, bf16[2,64,512]{2,1,0:T(8,128)(2,1)} %copy-done.10, ...), custom_call_target="tpu_custom_call" | custom-call | flops 1073741824 | bytes 1048576 | tf_op jit(solution)/shard_map/pallas_call | solution.py:309
  98.8 1.8 %all-to-all-done.2.refs_7_ = f32[16,1,1536]{2,1,0:T(1,128)S(1)} async-done(((f32[16,1,1536]{2,1,0:T(1,128)}), f32[16,1,1536]{2,1,0:T(1,128)S(1)}, u32[]{:S(2)}, u32[]{:S(2)}) %all-to-all-start.2) | async-done | bytes 98336 | tf_op jit(solution)/shard_map/all_to_all | solution.py:268
  100.6 3.4 %shard_map.101 = (f32[2,512]{1,0:T(2,128)}, bf16[2,8,8,8,512]{4,3,2,1,0:T(8,128)(2,1)}) custom-call(s32[1]{0:T(128)} %bitcast.me_ref, s32[8]{0:T(128)S(1)} %copy-done.16, bf16[2,2,64,512]{3,2,1,0:T(8,128)(2,1)S(1)} %get-tuple-element.19.refs_0_, bf16[2,2,64,512]{3,2,1,0:T(8,128)(2,1)S(1)} %collective-permute-done.1.refs_1_, ...), custom_call_target="tpu_custom_call" | custom-call | flops 1073741824 | bytes 1048576 | tf_op jit(solution)/shard_map/pallas_call | solution.py:331
  (43 shorter events, 0.1 us)
Async XLA Ops:
  0.6 40.6 %copy-start.17 = (s32[64]{0:T(128)S(1)}, s32[64]{0:T(128)}, u32[]{:S(2)}) copy-start(s32[64]{0:T(128)} %order_ref.3) | copy-start | bytes 772
  2.8 42.7 %copy-start.2 = (bf16[2,8,8,8,512]{4,3,2,1,0:T(8,128)(2,1)S(1)}, bf16[2,8,8,8,512]{4,3,2,1,0:T(8,128)(2,1)}, u32[]{:S(2)}) copy-start(bf16[2,8,8,8,512]{4,3,2,1,0:T(8,128)(2,1)} %mod_ref.1) | copy-start | bytes 3145732
  2.8 42.7 %copy-start.16 = (s32[8]{0:T(128)S(1)}, s32[8]{0:T(128)}, u32[]{:S(2)}) copy-start(s32[8]{0:T(128)} %slot_ref.3) | copy-start | bytes 100
  2.8 66.8 %copy-start = (bf16[2,512,512]{2,1,0:T(8,128)(2,1)S(1)}, bf16[2,512,512]{2,1,0:T(8,128)(2,1)}, u32[]{:S(2)}) copy-start(bf16[2,512,512]{2,1,0:T(8,128)(2,1)} %refs_5_.1) | copy-start | bytes 3145732
  2.8 38.4 %all-to-all-start = ((bf16[32,4,8,512]{3,2,1,0:T(8,128)(2,1)}), bf16[32,4,8,512]{3,2,1,0:T(8,128)(2,1)S(1)}, u32[]{:S(2)}, u32[]{:S(2)}) async-start(bf16[32,4,8,512]{3,2,1,0:T(8,128)(2,1)} %shard_map.95), calls=%async_computation | async-start | bytes 2097152 | tf_op jit(solution)/shard_map/all_to_all | solution.py:292
  42.7 4.3 %copy-start.3 = (bf16[4,2,64,512]{3,2,1,0:T(8,128)(2,1)}, bf16[4,2,64,512]{3,2,1,0:T(8,128)(2,1)S(1)}, u32[]{:S(2)}) copy-start(bf16[4,2,64,512]{3,2,1,0:T(8,128)(2,1)S(1)} %get-tuple-element.17.keep_ref) | copy-start | bytes 1572868
  42.7 36.7 %collective-permute-start = (bf16[4,2,64,512]{3,2,1,0:T(8,128)(2,1)}, bf16[4,2,64,512]{3,2,1,0:T(8,128)(2,1)}, u32[]{:S(2)}, u32[]{:S(2)}) collective-permute-start(bf16[4,2,64,512]{3,2,1,0:T(8,128)(2,1)} %get-tuple-element.18), channel_id=1, source_target_pairs={{0,128},{128,0},{1,129},{129,1},{2,130},{130,2},{3,131},{131,3},{4... | collective-permute-start | bytes 1572872 | tf_op jit(solution)/shard_map/ppermute | solution.py:263
  45.4 0.8 copy-start.13
  47.0 22.5 %copy-start.6 = (bf16[2,64,512]{2,1,0:T(8,128)(2,1)}, bf16[2,64,512]{2,1,0:T(8,128)(2,1)S(1)}, u32[]{:S(2)}) copy-start(bf16[2,64,512]{2,1,0:T(8,128)(2,1)S(1)} %get-tuple-element.25.refs_1_) | copy-start | bytes 393220
  47.0 22.5 %copy-start.7 = (bf16[2,64,512]{2,1,0:T(8,128)(2,1)}, bf16[2,64,512]{2,1,0:T(8,128)(2,1)S(1)}, u32[]{:S(2)}) copy-start(bf16[2,64,512]{2,1,0:T(8,128)(2,1)S(1)} %get-tuple-element.26.refs_2_) | copy-start | bytes 393220
  47.0 22.5 %copy-start.8 = (bf16[2,64,512]{2,1,0:T(8,128)(2,1)}, bf16[2,64,512]{2,1,0:T(8,128)(2,1)S(1)}, u32[]{:S(2)}) copy-start(bf16[2,64,512]{2,1,0:T(8,128)(2,1)S(1)} %get-tuple-element.27.refs_3_) | copy-start | bytes 393220
  47.1 22.5 %copy-start.9 = (bf16[2,64,512]{2,1,0:T(8,128)(2,1)}, bf16[2,64,512]{2,1,0:T(8,128)(2,1)S(1)}, u32[]{:S(2)}) copy-start(bf16[2,64,512]{2,1,0:T(8,128)(2,1)S(1)} %get-tuple-element.28.refs_4_) | copy-start | bytes 393220
  47.1 22.5 %copy-start.10 = (bf16[2,64,512]{2,1,0:T(8,128)(2,1)}, bf16[2,64,512]{2,1,0:T(8,128)(2,1)S(1)}, u32[]{:S(2)}) copy-start(bf16[2,64,512]{2,1,0:T(8,128)(2,1)S(1)} %get-tuple-element.29.refs_5_) | copy-start | bytes 393220
  47.1 22.5 %copy-start.11 = (bf16[2,64,512]{2,1,0:T(8,128)(2,1)}, bf16[2,64,512]{2,1,0:T(8,128)(2,1)S(1)}, u32[]{:S(2)}) copy-start(bf16[2,64,512]{2,1,0:T(8,128)(2,1)S(1)} %get-tuple-element.30.refs_6_) | copy-start | bytes 393220
  47.1 22.5 %copy-start.12 = (bf16[2,64,512]{2,1,0:T(8,128)(2,1)}, bf16[2,64,512]{2,1,0:T(8,128)(2,1)S(1)}, u32[]{:S(2)}) copy-start(bf16[2,64,512]{2,1,0:T(8,128)(2,1)S(1)} %get-tuple-element.31.refs_7_) | copy-start | bytes 393220
  47.1 26.8 %copy-start.5 = (bf16[2,64,512]{2,1,0:T(8,128)(2,1)}, bf16[2,64,512]{2,1,0:T(8,128)(2,1)S(1)}, u32[]{:S(2)}) copy-start(bf16[2,64,512]{2,1,0:T(8,128)(2,1)S(1)} %get-tuple-element.24.refs_0_) | copy-start | bytes 393220
  47.1 6.1 %collective-permute-start.4 = (bf16[2,64,512]{2,1,0:T(8,128)(2,1)S(1)}, bf16[2,64,512]{2,1,0:T(8,128)(2,1)S(1)}, u32[]{:S(2)}, u32[]{:S(2)}) collective-permute-start(bf16[2,64,512]{2,1,0:T(8,128)(2,1)S(1)} %get-tuple-element.25.refs_1_), channel_id=1, source_target_pairs={{0,32},{32,0},{64,96},{96,64},{128,160},{160,128},{192,224},{224,1... | collective-permute-start | bytes 393224 | tf_op jit(solution)/shard_map/ppermute | solution.py:263
  47.6 7.7 %collective-permute-start.5 = (bf16[2,64,512]{2,1,0:T(8,128)(2,1)S(1)}, bf16[2,64,512]{2,1,0:T(8,128)(2,1)S(1)}, u32[]{:S(2)}, u32[]{:S(2)}) collective-permute-start(bf16[2,64,512]{2,1,0:T(8,128)(2,1)S(1)} %get-tuple-element.26.refs_2_), channel_id=1, source_target_pairs={{0,64},{32,96},{64,0},{96,32},{128,192},{160,224},{192,128},{224,1... | collective-permute-start | bytes 393224 | tf_op jit(solution)/shard_map/ppermute | solution.py:263
  50.2 7.4 %collective-permute-start.6 = (bf16[2,64,512]{2,1,0:T(8,128)(2,1)S(1)}, bf16[2,64,512]{2,1,0:T(8,128)(2,1)S(1)}, u32[]{:S(2)}, u32[]{:S(2)}) collective-permute-start(bf16[2,64,512]{2,1,0:T(8,128)(2,1)S(1)} %get-tuple-element.27.refs_3_), channel_id=1, source_target_pairs={{0,96},{32,64},{64,32},{96,0},{128,224},{160,192},{192,160},{224,1... | collective-permute-start | bytes 393224 | tf_op jit(solution)/shard_map/ppermute | solution.py:263
  50.7 11.4 %collective-permute-start.7 = (bf16[2,64,512]{2,1,0:T(8,128)(2,1)S(1)}, bf16[2,64,512]{2,1,0:T(8,128)(2,1)S(1)}, u32[]{:S(2)}, u32[]{:S(2)}) collective-permute-start(bf16[2,64,512]{2,1,0:T(8,128)(2,1)S(1)} %get-tuple-element.28.refs_4_), channel_id=1, source_target_pairs={{0,128},{32,160},{64,192},{96,224},{128,0},{160,32},{192,64},{224,... | collective-permute-start | bytes 393224 | tf_op jit(solution)/shard_map/ppermute | solution.py:263
  53.3 11.2 %collective-permute-start.8 = (bf16[2,64,512]{2,1,0:T(8,128)(2,1)S(1)}, bf16[2,64,512]{2,1,0:T(8,128)(2,1)S(1)}, u32[]{:S(2)}, u32[]{:S(2)}) collective-permute-start(bf16[2,64,512]{2,1,0:T(8,128)(2,1)S(1)} %get-tuple-element.29.refs_5_), channel_id=1, source_target_pairs={{0,160},{32,128},{64,224},{96,192},{128,32},{160,0},{192,96},{224,... | collective-permute-start | bytes 393224 | tf_op jit(solution)/shard_map/ppermute | solution.py:263
  55.3 13.5 %collective-permute-start.9 = (bf16[2,64,512]{2,1,0:T(8,128)(2,1)S(1)}, bf16[2,64,512]{2,1,0:T(8,128)(2,1)S(1)}, u32[]{:S(2)}, u32[]{:S(2)}) collective-permute-start(bf16[2,64,512]{2,1,0:T(8,128)(2,1)S(1)} %get-tuple-element.30.refs_6_), channel_id=1, source_target_pairs={{0,192},{32,224},{64,128},{96,160},{128,64},{160,96},{192,0},{224,... | collective-permute-start | bytes 393224 | tf_op jit(solution)/shard_map/ppermute | solution.py:263
  57.6 11.9 %collective-permute-start.10 = (bf16[2,64,512]{2,1,0:T(8,128)(2,1)S(1)}, bf16[2,64,512]{2,1,0:T(8,128)(2,1)S(1)}, u32[]{:S(2)}, u32[]{:S(2)}) collective-permute-start(bf16[2,64,512]{2,1,0:T(8,128)(2,1)S(1)} %get-tuple-element.31.refs_7_), channel_id=1, source_target_pairs={{0,224},{32,192},{64,160},{96,128},{128,96},{160,64},{192,32},{224... | collective-permute-start | bytes 393224 | tf_op jit(solution)/shard_map/ppermute | solution.py:263
  69.6 9.8 %copy-start.4 = (bf16[4,2,64,512]{3,2,1,0:T(8,128)(2,1)S(1)}, bf16[4,2,64,512]{3,2,1,0:T(8,128)(2,1)}, u32[]{:S(2)}) copy-start(bf16[4,2,64,512]{3,2,1,0:T(8,128)(2,1)} %copy-done.3) | copy-start | bytes 1572868
  74.6 13.1 %all-to-all-start.1 = ((f32[16,1,1536]{2,1,0:T(1,128)}), f32[16,1,1536]{2,1,0:T(1,128)S(1)}, u32[]{:S(2)}, u32[]{:S(2)}) async-start(f32[16,1,1536]{2,1,0:T(1,128)} %broadcast_in_dim.14), calls=%async_computation.1 | async-start | bytes 196608 | tf_op jit(solution)/shard_map/all_to_all | solution.py:268
  81.2 19.3 %collective-permute-start.1 = (bf16[2,2,64,512]{3,2,1,0:T(8,128)(2,1)}, bf16[2,2,64,512]{3,2,1,0:T(8,128)(2,1)S(1)}, u32[]{:S(2)}, u32[]{:S(2)}) collective-permute-start(bf16[2,2,64,512]{3,2,1,0:T(8,128)(2,1)} %get-tuple-element.20), channel_id=1, source_target_pairs={{0,32},{32,0},{64,96},{96,64},{1,33},{33,1},{65,97},{97,65},{2,34}... | collective-permute-start | bytes 786440 | tf_op jit(solution)/shard_map/ppermute | solution.py:263
  82.6 18.0 %collective-permute-start.2 = (bf16[2,2,64,512]{3,2,1,0:T(8,128)(2,1)}, bf16[2,2,64,512]{3,2,1,0:T(8,128)(2,1)S(1)}, u32[]{:S(2)}, u32[]{:S(2)}) collective-permute-start(bf16[2,2,64,512]{3,2,1,0:T(8,128)(2,1)} %get-tuple-element.21), channel_id=1, source_target_pairs={{0,64},{32,96},{64,0},{96,32},{1,65},{33,97},{65,1},{97,33},{2,66}... | collective-permute-start | bytes 786440 | tf_op jit(solution)/shard_map/ppermute | solution.py:263
  82.6 18.0 %collective-permute-start.3 = (bf16[2,2,64,512]{3,2,1,0:T(8,128)(2,1)S(1)}, bf16[2,2,64,512]{3,2,1,0:T(8,128)(2,1)S(1)}, u32[]{:S(2)}, u32[]{:S(2)}) collective-permute-start(bf16[2,2,64,512]{3,2,1,0:T(8,128)(2,1)S(1)} %get-tuple-element.22), channel_id=1, source_target_pairs={{0,96},{32,64},{64,32},{96,0},{1,97},{33,65},{65,33},{97,1},{2,98}... | collective-permute-start | bytes 786440 | tf_op jit(solution)/shard_map/ppermute | solution.py:263
  88.4 12.1 %all-to-all-start.2 = ((f32[16,1,1536]{2,1,0:T(1,128)}), f32[16,1,1536]{2,1,0:T(1,128)S(1)}, u32[]{:S(2)}, u32[]{:S(2)}) async-start(f32[16,1,1536]{2,1,0:T(1,128)} %broadcast_in_dim.15), calls=%async_computation.2 | async-start | bytes 196608 | tf_op jit(solution)/shard_map/all_to_all | solution.py:268
  94.3 6.3 %copy-start.1 = (bf16[2,512,512]{2,1,0:T(8,128)(2,1)S(1)}, bf16[2,512,512]{2,1,0:T(8,128)(2,1)}, u32[]{:S(2)}) copy-start(bf16[2,512,512]{2,1,0:T(8,128)(2,1)} %refs_5_.1) | copy-start | bytes 3145732
  94.3 6.3 %copy-start.14 = (f32[2,512]{1,0:T(2,128)S(1)}, f32[2,512]{1,0:T(2,128)}, u32[]{:S(2)}) copy-start(f32[2,512]{1,0:T(2,128)} %refs_8_.3) | copy-start | bytes 12292
  94.3 6.3 %copy-start.15 = (f32[512]{0:T(512)S(1)}, f32[512]{0:T(512)}, u32[]{:S(2)}) copy-start(f32[512]{0:T(512)} %param.15) | copy-start | bytes 6148
